TPU v7x, 8 devices: a whole 2x2x1 slice. The times are simulated.
8 devices in a mesh: vp: 8 (over z, y, x, core).
Axes of the slice: x: 2, y: 2, z: 1, core: 2. Of those that a mesh axis runs over, the one named last changes fastest.
Arguments:
- residual: bfloat16 [1024, 1024], replicated
- labels: int32 [1024], replicated
- loss_mask: float32 [1024], replicated
- norm_gain: float32 [1024], replicated
- embed_table: bfloat16 [49408, 1024], P('vp')
Outputs:
- output 1: float32 [], replicated
- output 2: float32 [1024, 1024], P('vp')
- output 3: float32 [49408, 1024], P('vp')
- output 4: float32 [1024], replicated
All inputs are finite; a program needn't handle non-finite values.
Results may differ from a plain program's by a relative error of at most 0.001.
Values sent between devices are 32-bit elements.
A program may use at most 1 GiB of HBM per device.

v0:
```python
import jax
import jax.numpy as jnp
from jax import lax
from jax.sharding import PartitionSpec as P

VOCAB_REAL = 49155
LOGIT_SCALE = 6.0
NORM_EPS = 1e-6


def solution(mesh):
    vp_axis = mesh.axis_names[0]
    group_size = mesh.shape[vp_axis]

    def local_step(residual, labels, loss_mask, norm_gain, table_shard):
        tokens = residual.shape[0]
        shard_rows = table_shard.shape[0]
        tok_rows = tokens // group_size
        my_index = lax.axis_index(vp_axis)
        x_f32 = residual.astype(jnp.float32)
        inv_rms = lax.rsqrt(jnp.mean(x_f32 * x_f32, axis=-1, keepdims=True) + NORM_EPS)
        x_hat = x_f32 * inv_rms
        hidden = (x_hat * norm_gain).astype(jnp.bfloat16)
        logits = jnp.einsum('td,vd->tv', hidden, table_shard, preferred_element_type=jnp.float32) / LOGIT_SCALE
        col_ids = my_index * shard_rows + lax.broadcasted_iota(jnp.int32, (1, shard_rows), 1)
        logits = jnp.where(col_ids < VOCAB_REAL, logits, -jnp.inf)
        row_max = lax.pmax(jnp.max(logits, axis=-1), vp_axis)
        shifted = jnp.exp(logits - row_max[:, None])
        is_label = col_ids == labels[:, None]
        part_stats = jnp.stack([jnp.sum(shifted, axis=-1), jnp.sum(jnp.where(is_label, logits, 0.0), axis=-1)])
        row_stats = lax.psum(part_stats, vp_axis)
        sum_exp = row_stats[0]
        log_norm = row_max + jnp.log(sum_exp)
        mask_total = jnp.sum(loss_mask)
        tok_weight = loss_mask / mask_total
        mean_loss = jnp.sum(loss_mask * (log_norm - row_stats[1])) / mask_total
        row_prob = shifted / sum_exp[:, None]
        d_logits = (jnp.where(is_label, row_prob - 1.0, row_prob) * tok_weight[:, None]).astype(jnp.bfloat16)
        d_part = jnp.dot(d_logits, table_shard, preferred_element_type=jnp.float32) / LOGIT_SCALE
        d_embed = jnp.einsum('tv,td->vd', d_logits, hidden, preferred_element_type=jnp.float32) / LOGIT_SCALE
        d_hidden = lax.psum_scatter(d_part, vp_axis, scatter_dimension=0, tiled=True)
        x_hat_loc = lax.dynamic_slice_in_dim(x_hat, my_index * tok_rows, tok_rows, axis=0)
        inv_loc = lax.dynamic_slice_in_dim(inv_rms, my_index * tok_rows, tok_rows, axis=0)
        d_gain = lax.psum(jnp.sum(d_hidden * x_hat_loc, axis=0), vp_axis)
        value_a6 = d_hidden * norm_gain
        d_residual = inv_loc * (value_a6 - x_hat_loc * jnp.mean(value_a6 * x_hat_loc, axis=-1, keepdims=True))
        return mean_loss, d_residual, d_embed, d_gain

    return jax.shard_map(local_step, mesh=mesh, in_specs=(P(), P(), P(), P(), P(vp_axis, None)), out_specs=(P(), P(vp_axis, None), P(vp_axis, None), P()), check_vma=False)
```

profile of v0, /device:TPU:0, one launch (start us, length us, event | category | flops | bytes accessed | tf_op | source)
XLA Modules:
  0.0 206.8 jit_solution(2274079935590038733)
XLA Ops:
  7.2 0.0 reduce-scatter.2.cloned.1.call-start
  7.2 2.1 %fusion.4 = f32[1024]{0:T(1024)S(1)} fusion(bf16[1024,1024]{1,0:T(8,128)(2,1)} %param.5), kind=kLoop, calls=%fused_computation.11 | loop fusion | flops 3144704 | bytes 2101248 | tf_op jit(solution)/shard_map/reduce_sum | solution.py:21
  9.3 0.0 copy-start.2
  9.3 23.3 %fusion.7 = (f32[1024]{0:T(1024)S(1)}, f32[1024,6176]{0,1:T(8,128)}) fusion(bf16[6176,1024]{1,0:T(8,128)(2,1)} %param.9, f32[1024]{0:T(1024)} %param.8, f32[1024]{0:T(1024)S(1)} %add_rsqrt_fusion, bf16[1024,1024]{1,0:T(8,128)(2,1)} %param.5, pred[6176]{0:T(1024)(128)(4,1)S(1)} %broadcast_compare_fusion), kind=kOutput, calls=%fused_computation.26 | convolution fusion | flops 12975176704 | bytes 40060960 | tf_op jit(solution)/shard_map/td,vd->tv/dot_general | solution.py:24
  32.7 25.1 %pmax.7 = f32[1024]{0:T(1024)S(1)} all-reduce(f32[1024]{0:T(1024)S(1)} %get-tuple-element.12), channel_id=1, replica_groups=mesh['vp'=8] {'vp'}, use_global_device_ids=true, to_apply=%region_2.3 | all-reduce | flops 1024 | bytes 8192 | tf_op jit(solution)/shard_map/pmax | solution.py:27
  57.7 0.0 copy-done.2
  57.8 0.0 copy-start.4
  57.8 11.6 %fusion.3 = (f32[1024]{0:T(1024)S(1)}, f32[1024]{0:T(1024)S(1)}) fusion(f32[1024,6176]{0,1:T(8,128)} %get-tuple-element.13, f32[1024]{0:T(1024)S(1)} %pmax.7, s32[1024]{0:T(1024)S(1)} %copy-done.2, s32[6176]{0:T(1024)S(1)} %iota_add_fusion), kind=kLoop, calls=%fused_computation.7 | loop fusion | flops 31619072 | bytes 25337984 | tf_op jit(solution)/shard_map/reduce_sum | solution.py:30
  69.4 23.3 %psum.14 = f32[2,1024]{1,0:T(2,128)S(1)} all-reduce(f32[2,1024]{1,0:T(2,128)S(1)} %pad_maximum_fusion), channel_id=1, replica_groups=mesh['vp'=8] {'vp'}, use_global_device_ids=true, to_apply=%region_5.6 | all-reduce | flops 2048 | bytes 16384 | tf_op jit(solution)/shard_map/psum | solution.py:31
  92.7 0.0 copy-done.4
  92.7 0.6 fusion.5
  93.3 0.6 broadcast_divide_fusion
  94.0 12.3 %fusion.2 = bf16[1024,6176]{0,1:T(8,128)(2,1)S(1)} fusion(f32[1024,6176]{0,1:T(8,128)} %get-tuple-element.13, f32[1024]{0:T(1024)S(1)} %broadcast_divide_fusion, f32[1024]{0:T(1024)S(1)} %bitcast.9, s32[1024]{0:T(1024)S(1)} %copy-done.2, f32[1024]{0:T(1024)S(1)} %pmax.7, s32[6176]{0:T(1024)S(1)} %iota_add_fusion), kind=kLoop, calls=%fused_computation.4 | loop fusion | flops 44269568 | bytes 37986432 | tf_op jit(solution)/shard_map/convert_element_type | solution.py:38
  106.3 0.0 copy-start
  106.3 4.6 %copy-done = bf16[1024,6176]{0,1:T(8,128)(2,1)} copy-done((bf16[1024,6176]{0,1:T(8,128)(2,1)}, bf16[1024,6176]{0,1:T(8,128)(2,1)S(1)}, u32[]{:S(2)}) %copy-start) | copy-done | bytes 12648472
  110.9 0.0 copy-start.1
  110.9 0.0 copy-start.3
  110.9 17.8 %convolution_multiply_fusion.1 = f32[1024,1024]{1,0:T(8,128)} fusion(bf16[1024,6176]{0,1:T(8,128)(2,1)S(1)} %fusion.2, bf16[6176,1024]{1,0:T(8,128)(2,1)} %param.9), kind=kOutput, calls=%fused_computation.13 | convolution fusion | flops 12953059328 | bytes 29491200 | tf_op jit(solution)/shard_map/dot_general | solution.py:39
  128.6 0.0 reduce-scatter.2.cloned.1.call-update
  130.0 0.1 dynamic-slice.3
  130.1 0.0 copy-done.1
  130.1 2.3 %convert_multiply_fusion = f32[1024,1024]{1,0:T(8,128)} fusion(bf16[1024,1024]{1,0:T(8,128)(2,1)S(1)} %copy-done.1, f32[1024]{0:T(1024)S(1)} %add_rsqrt_fusion), kind=kLoop, calls=%fused_computation.9 | loop fusion | flops 2097152 | bytes 6295552 | tf_op jit(solution)/shard_map/mul | solution.py:22
  132.4 0.0 copy-done.3
  132.4 21.4 %convolution_multiply_fusion = f32[6176,1024]{1,0:T(8,128)} fusion(bf16[1024,6176]{0,1:T(8,128)(2,1)} %copy-done, f32[1024]{0:T(1024)S(1)} %copy-done.3, bf16[1024,1024]{1,0:T(8,128)(2,1)S(1)} %copy-done.1, f32[1024]{0:T(1024)S(1)} %add_rsqrt_fusion), kind=kOutput, calls=%fused_computation.8 | convolution fusion | flops 12962529280 | bytes 40050688 | tf_op jit(solution)/shard_map/tv,td->vd/dot_general | solution.py:40
  153.8 19.3 %reduce-scatter.2.cloned.1.call-done = f32[128,1024]{1,0:T(8,128)} async-done(((f32[1024,1024]{1,0:T(8,128)}), f32[128,1024]{1,0:T(8,128)}) %reduce-scatter.2.cloned.1.call-update) | async-done | bytes 524304 | tf_op jit(solution)/shard_map/reduce_scatter | solution.py:41
  173.0 1.4 multiply_reduce_fusion
  174.4 22.3 %psum.15 = f32[1024]{0:T(1024)} all-reduce(f32[1024]{0:T(1024)S(1)} %get-tuple-element.6), channel_id=1, replica_groups=mesh['vp'=8] {'vp'}, use_global_device_ids=true, to_apply=%region_11.12 | all-reduce | flops 1024 | bytes 8192 | tf_op jit(solution)/shard_map/psum | solution.py:44
  196.7 2.1 %subtract_multiply_fusion = f32[128,1024]{1,0:T(8,128)} fusion(f32[128,1024]{1,0:T(8,128)} %reduce-scatter.2.cloned.1.call-done, f32[1024,1024]{1,0:T(8,128)} %convert_multiply_fusion, s32[]{:T(128)S(6)} %select_n.18, f32[128]{0:T(128)S(1)} %broadcast_multiply_fusion, f32[1024]{0:T(1024)S(1)} %copy-done.3, f32[128]{0:T(128)S(1)} %dynamic-slice.3), kind=kLoop, calls=%fused_computation.15 | loop fusion | flops 524288 | bytes 1577988 | tf_op jit(solution)/shard_map/mul | solution.py:46
  (6 shorter events, 0.1 us)
Async XLA Ops:
  7.2 165.9 %reduce-scatter.2.cloned.1.call-start = ((), (), s32[]{:S(2)}) async-start(), calls=%async_computation.1 | async-start | bytes 4718592 | tf_op jit(solution)/shard_map/reduce_scatter | solution.py:41
  9.3 48.4 %copy-start.2 = (s32[1024]{0:T(1024)S(1)}, s32[1024]{0:T(1024)}, u32[]{:S(2)}) copy-start(s32[1024]{0:T(1024)} %param.6) | copy-start | bytes 12292
  57.8 35.0 %copy-start.4 = (f32[1024]{0:T(1024)S(1)}, f32[1024]{0:T(1024)}, u32[]{:S(2)}) copy-start(f32[1024]{0:T(1024)} %param.7) | copy-start | bytes 12292
  106.3 4.6 %copy-start = (bf16[1024,6176]{0,1:T(8,128)(2,1)}, bf16[1024,6176]{0,1:T(8,128)(2,1)S(1)}, u32[]{:S(2)}) copy-start(bf16[1024,6176]{0,1:T(8,128)(2,1)S(1)} %fusion.2) | copy-start | bytes 37945348
  110.9 19.2 %copy-start.1 = (bf16[1024,1024]{1,0:T(8,128)(2,1)S(1)}, bf16[1024,1024]{1,0:T(8,128)(2,1)}, u32[]{:S(2)}) copy-start(bf16[1024,1024]{1,0:T(8,128)(2,1)} %param.5) | copy-start | bytes 6291460
  110.9 21.5 %copy-start.3 = (f32[1024]{0:T(1024)S(1)}, f32[1024]{0:T(1024)}, u32[]{:S(2)}) copy-start(f32[1024]{0:T(1024)} %param.8) | copy-start | bytes 12292
Sparse Core Ops, SparseCore 0:
  128.8 44.1 reduce-scatter.1
where the time goes:
time: 207 us
  blocking collectives  70.6 us (34%)
  matrix products  62.5 us (30%)
  other arithmetic  33.1 us (16%)
  waiting for transfers between devices  19.3 us (9%)
  between operations  16.6 us (8%)
  local copies, waits for them, and re-layouts  4.66 us (2%)
    pmax x1, blocking collectives, local_step(): row_max = lax.pmax(jnp.max(logits, axis=-1), vp_axis)  25.1 us
    dot_general x1, matrix products, local_step(): jnp.einsum('td,vd->tv', hidden, table_shard, preferred_element_type=jnp.f...  23.3 us
    psum x1, blocking collectives, local_step(): row_stats = lax.psum(part_stats, vp_axis)  23.3 us
    psum x1, blocking collectives, local_step(): d_gain = lax.psum(jnp.sum(d_hidden * x_hat_loc, axis=0), vp_axis)  22.3 us
    dot_general x1, matrix products, local_step(): jnp.einsum('tv,td->vd', d_logits, hidden, preferred_element_type=jnp.floa...  21.4 us
    reduce_scatter x1, waiting for transfers between devices, local_step(): lax.psum_scatter(d_part, vp_axis, scatter_dimension=0, tiled=True)  19.3 us
    dot_general x1, matrix products, local_step(): jnp.dot(d_logits, table_shard, preferred_element_type=jnp.float32)  17.8 us
    convert_element_type x1, other arithmetic, local_step(): (jnp.where(is_label, row_prob - 1.0, row_prob) * tok_weight[:, None]).ast...  12.3 us
  transfers between devices with their start and end apart: 1, of which 1 were waited for; matrix products, arithmetic and copies ran while one was open for 11% of the time, Pallas kernels for 0%

commit v1 on v0

v1 whole, which is shorter than its diff:
```python
import functools

import jax
import jax.numpy as jnp
from jax import lax
from jax.experimental import pallas as pl
from jax.experimental.pallas import tpu as pltpu
from jax.sharding import PartitionSpec as P

VOCAB_REAL = 49155
LOGIT_SCALE = 6.0
NORM_EPS = 1e-6
LOG2E = 1.4426950408889634
F32 = jnp.float32
BF16 = jnp.bfloat16
MESH = pl.DeviceIdType.MESH

N_DEV = 8
TOKENS = 1024
DIM = 1024
ROWS = 6176
CHUNKS = 4
CTOK = 256
PIECE = 32
HALF = DIM // 2
L_TILE = 256
K_TILE = 1024
DZ_BLOCK = 16
MASK_FROM = VOCAB_REAL - (N_DEV - 1) * ROWS
EXP_SCALE = LOG2E / LOGIT_SCALE


def split_rows(step):
    cuts = [[i * step, step] for i in range(ROWS // step)]
    cuts[-1][1] = ROWS - cuts[-1][0]
    return [tuple(c) for c in cuts]


TILES = split_rows(L_TILE)
KTILES = split_rows(K_TILE)
N_TILES = len(TILES)


def fold8(v):
    return jnp.sum(v.reshape(v.shape[0] // 8, 8, v.shape[1]), axis=0)


def interleave(main, side, ratio):
    main_done = side_done = False
    while not (main_done and side_done):
        if not main_done:
            main_done = next(main, 0) == 0
        for _ in range(ratio):
            if not side_done:
                side_done = next(side, 0) == 0


def main_kernel(x_hbm, y_in, m_in, g_in, e_hbm,
                dz_hbm, h_hbm, dx_out, dg_out, loss_out,
                emb, xv, hs, ht, rcol, ebuf, dzb, acc, ub0, ub1, yrow, mrow,
                tmax, tsum, crow, tgt, stx, srx, lossv, dgv, dgrx, ra, rb, rc,
                in_sem, h_sem, dz_sem, st_send, st_recv, rs_send, rs_recv, dg_send, dg_recv):
    me = lax.axis_index("vp")
    core = lax.rem(me, 2)
    xc = lax.rem(me // 2, 2)
    yc = me // 4
    peer_core = me + 1 - 2 * core
    peer_x = me + 2 - 4 * xc
    peer_y = me + 4 - 8 * yc

    mid_row = TILES[N_TILES // 2][0]
    e_copies = [
        pltpu.make_async_copy(e_hbm.at[pl.ds(0, mid_row)], emb.at[pl.ds(0, mid_row)], in_sem.at[0]),
        pltpu.make_async_copy(e_hbm.at[pl.ds(mid_row, ROWS - mid_row)], emb.at[pl.ds(mid_row, ROWS - mid_row)], in_sem.at[1]),
    ]
    x_copies = [pltpu.make_async_copy(x_hbm.at[:, c], xv.at[c], in_sem.at[2 + c]) for c in range(CHUNKS)]
    x_copies[0].start()
    e_copies[0].start()
    e_copies[1].start()
    for c in range(1, CHUNKS):
        x_copies[c].start()

    barrier = pltpu.get_barrier_semaphore()
    for k in range(1, N_DEV):
        pl.semaphore_signal(barrier, inc=1, device_id=(lax.rem(me + k, N_DEV),), device_id_type=MESH)

    lane = lax.broadcasted_iota(jnp.int32, (1, 128), 1) // PIECE
    base = me * ROWS
    for c in range(CHUNKS):
        for half in range(2):
            yh = jnp.zeros((1, 128), jnp.int32)
            mh = jnp.zeros((1, 128), F32)
            for i in range(4):
                row = half * 4 + i
                shift = (PIECE * (i - c)) % 128
                yr, mr = y_in[row:row + 1, :], m_in[row:row + 1, :]
                if shift:
                    yr, mr = pltpu.roll(yr, shift, 1), pltpu.roll(mr, shift, 1)
                yh = jnp.where(lane == i, yr, yh)
                mh = jnp.where(lane == i, mr, mh)
            yrow[c, :, half * 128:half * 128 + 128] = yh - base
            mrow[c, :, half * 128:half * 128 + 128] = mh
    mask_total = jnp.sum(jnp.sum(m_in[...], axis=0, keepdims=True), axis=1, keepdims=True)
    lossv[...] = jnp.zeros_like(lossv)
    dgv[...] = jnp.zeros_like(dgv)
    limit = VOCAB_REAL - base

    def norm_chunk(c):
        g = g_in[...]
        for r in range(CTOK // PIECE):
            xf = xv[c, r].astype(F32)
            inv = lax.rsqrt(jnp.mean(xf * xf, axis=1, keepdims=True) + NORM_EPS)
            rcol[c, r] = jnp.broadcast_to(inv, (PIECE, 128))
            hs[c, r * PIECE:(r + 1) * PIECE, :] = (xf * inv * g).astype(BF16)
        ht[c] = hs[c].T

    def logits(c, lo, hi, tg):
        slot = lax.rem(c, 2)
        iota = lax.broadcasted_iota(jnp.int32, (8, CTOK), 0)
        y = yrow[c]
        eb = ebuf.at[slot]
        ubs = (ub0, ub1)
        state = [tg]

        def mm(i):
            s, n = TILES[i]
            ubs[i % 2][0:n, :] = jnp.dot(emb[s:s + n, :], ht[c], preferred_element_type=F32)
            yield 1

        def post(i):
            s, n = TILES[i]
            u_ref = ubs[i % 2]
            m8 = jnp.full((8, CTOK), -jnp.inf, F32)
            for r in range(0, n, 8):
                u = u_ref[r:r + 8, :]
                if s + r + 8 > MASK_FROM:
                    u = jnp.where(iota < limit - (s + r), u, -jnp.inf)
                    u_ref[r:r + 8, :] = u
                m8 = jnp.maximum(m8, u)
            m = jnp.max(m8, axis=0, keepdims=True)
            s8 = jnp.zeros((8, CTOK), F32)
            for r in range(0, n, 8):
                u = u_ref[r:r + 8, :]
                e = jnp.exp2((u - m) * EXP_SCALE)
                eb[s + r:s + r + 8, :] = e
                s8 = s8 + e
                state[0] = state[0] + jnp.where(iota == (y - (s + r)), u, 0.0)
                if r % 64 == 56:
                    yield 1
            tmax[slot, i:i + 1, :] = m
            tsum[slot, i:i + 1, :] = jnp.sum(s8, axis=0, keepdims=True)
            yield 1

        for _ in mm(lo):
            pass
        for i in range(lo + 1, hi):
            interleave(mm(i), post(i - 1), 6)
        for _ in post(hi - 1):
            pass
        return state[0]

    def stat_copy(c, k):
        return pltpu.make_async_remote_copy(
            src_ref=stx.at[c], dst_ref=srx.at[c, k], send_sem=st_send.at[c, k], recv_sem=st_recv.at[c, k],
            device_id=(lax.rem(me + k, N_DEV),), device_id_type=MESH)

    def send_stats(c, tg):
        slot = lax.rem(c, 2)
        tm = tmax[slot]
        m_loc = jnp.max(tm, axis=0, keepdims=True)
        s_loc = jnp.sum(tsum[slot] * jnp.exp2((tm - m_loc) * EXP_SCALE), axis=0, keepdims=True)
        stx[c, 0:1, :] = m_loc
        stx[c, 1:2, :] = s_loc
        stx[c, 2:3, :] = jnp.sum(tg, axis=0, keepdims=True)
        for k in range(1, N_DEV):
            stat_copy(c, k).start()

    def recv_stats(c):
        slot = lax.rem(c, 2)
        for k in range(1, N_DEV):
            stat_copy(c, k).wait()
        parts = [stx[c]] + [srx[c, k] for k in range(1, N_DEV)]
        m_all = functools.reduce(jnp.maximum, [p[0:1] for p in parts])
        s_all = functools.reduce(jnp.add, [p[1:2] * jnp.exp2((p[0:1] - m_all) * EXP_SCALE) for p in parts])
        t_all = functools.reduce(jnp.add, [p[2:3] for p in parts])
        mask = mrow[c]
        weight = mask / mask_total
        lossv[...] += mask * (m_all / LOGIT_SCALE + jnp.log(s_all) - t_all / LOGIT_SCALE)
        crow[...] = jnp.exp2((tmax[slot] - m_all) * EXP_SCALE) * (weight / s_all)
        return weight

    def dz_out(c):
        return pltpu.make_async_copy(dzb.at[lax.rem(c, 2)], dz_hbm.at[:, pl.ds(pl.multiple_of(c * CTOK, CTOK), CTOK)], dz_sem.at[lax.rem(c, 2)])

    def dz_rows(c, weight, k):
        slot = lax.rem(c, 2)
        iota = lax.broadcasted_iota(jnp.int32, (DZ_BLOCK, CTOK), 0)
        y = yrow[c]
        s0, n0 = KTILES[k]
        for i, (s, n) in enumerate(TILES):
            if s0 <= s < s0 + n0:
                ci = crow[i:i + 1, :]
                for r in range(s, s + n, DZ_BLOCK):
                    e = ebuf[slot, r:r + DZ_BLOCK, :]
                    dzb[slot, r:r + DZ_BLOCK, :] = (e * ci - jnp.where(iota == (y - r), weight, 0.0)).astype(BF16)

    def dh_mm(c, k, half):
        s, n = KTILES[k]
        cols = slice(half * HALF, half * HALF + HALF)
        part = lax.dot_general(dzb[lax.rem(c, 2), s:s + n, :], emb[s:s + n, cols], (((0,), (0,)), ((), ())), preferred_element_type=F32)
        part = part.reshape(2, 2, 2, PIECE, HALF)
        if k == 0:
            acc[c, :, :, :, :, cols] = part
        else:
            acc[c, :, :, :, :, cols] += part

    def dg_part(c, half):
        cols = slice(half * HALF, half * HALF + HALF)
        total = jnp.zeros((8, HALF), F32)
        for r in range(CTOK // PIECE):
            inv = rcol[c, r][:, 0:1]
            xh = xv[c, r, :, cols].astype(F32) * inv
            total = total + fold8(acc[c, r // 4, (r // 2) % 2, r % 2, :, cols] * xh)
        dgv[:, cols] += jnp.sum(total, axis=0, keepdims=True)

    def rs_copy(c, half, stage):
        cols = pl.ds(half * HALF, HALF)
        if stage == 0:
            src, dst, dev = acc.at[c, :, :, 1 - core, :, cols], ra.at[c, half], peer_core
        elif stage == 1 and half == 0:
            src, dst, dev = acc.at[c, :, 1 - xc, core, :, cols], rb.at[c, half], peer_x
        elif stage == 1:
            src, dst, dev = acc.at[c, 1 - yc, :, core, :, cols], rb.at[c, half], peer_y
        elif half == 0:
            src, dst, dev = acc.at[c, 1 - yc, xc, core, :, cols], rc.at[c, half], peer_y
        else:
            src, dst, dev = acc.at[c, yc, 1 - xc, core, :, cols], rc.at[c, half], peer_x
        return pltpu.make_async_remote_copy(
            src_ref=src, dst_ref=dst, send_sem=rs_send.at[c, half, stage], recv_sem=rs_recv.at[c, half, stage],
            device_id=(dev,), device_id_type=MESH)

    def rs_start(c, half, stage):
        rs_copy(c, half, stage).start()

    def rs_finish(c, half, stage):
        rs_copy(c, half, stage).wait()
        cols = pl.ds(half * HALF, HALF)
        if stage == 0:
            acc[c, :, :, core, :, cols] += ra[c, half]
        elif stage == 1 and half == 0:
            acc[c, :, xc, core, :, cols] += rb[c, half]
        elif stage == 1:
            acc[c, yc, :, core, :, cols] += rb[c, half]
        else:
            acc[c, yc, xc, core, :, cols] += rc[c, half]
        if stage < 2:
            rs_start(c, half, stage + 1)

    def step(s, _):
        lc = jnp.minimum(s, CHUNKS - 1)
        dc = jnp.maximum(s - 1, 0)
        pc = jnp.maximum(s - 2, 0)

        @pl.when(s < CHUNKS)
        def _():
            tgt[...] = logits(lc, 0, N_TILES // 2, jnp.zeros((8, CTOK), F32))

        @pl.when(s == 0)
        def _():
            e_copies[1].wait()
            for c in range(1, CHUNKS):
                x_copies[c].wait()

        @pl.when(jnp.logical_and(s >= 2, s < CHUNKS))
        def _():
            rs_finish(pc, 1, 0)

        @pl.when(s < CHUNKS)
        def _():
            tg = logits(lc, N_TILES // 2, N_TILES, tgt[...])
            send_stats(lc, tg)

        @pl.when(s < CHUNKS - 1)
        def _():
            norm_chunk(s + 1)

        @pl.when(jnp.logical_and(s >= 2, s < CHUNKS))
        def _():
            rs_finish(pc, 0, 1)

        @pl.when(s >= 1)
        def _():
            @pl.when(s >= 3)
            def _():
                dz_out(dc).wait()
            weight = recv_stats(dc)
            dz_rows(dc, weight, 0)
            for k in range(1, len(KTILES)):
                dz_rows(dc, weight, k)
                dh_mm(dc, k - 1, 0)
            dh_mm(dc, len(KTILES) - 1, 0)
            dz_out(dc).start()
            rs_start(dc, 0, 0)
            dg_part(dc, 0)

        @pl.when(jnp.logical_and(s >= 2, s < CHUNKS))
        def _():
            rs_finish(pc, 1, 1)

        @pl.when(s == CHUNKS)
        def _():
            rs_finish(pc, 1, 0)

        @pl.when(s >= 1)
        def _():
            for k in range(len(KTILES)):
                dh_mm(dc, k, 1)
            rs_start(dc, 1, 0)
            rs_finish(dc, 0, 0)
            dg_part(dc, 1)

        @pl.when(jnp.logical_and(s >= 2, s < CHUNKS))
        def _():
            rs_finish(pc, 0, 2)
            rs_finish(pc, 1, 2)
        return 0

    x_copies[0].wait()
    norm_chunk(0)
    pl.semaphore_wait(barrier, N_DEV - 1)
    e_copies[0].wait()
    lax.fori_loop(0, CHUNKS + 1, step, 0)

    def dg_copy(k):
        return pltpu.make_async_remote_copy(
            src_ref=dgv, dst_ref=dgrx.at[k], send_sem=dg_send.at[k], recv_sem=dg_recv.at[k],
            device_id=(lax.rem(me + k, N_DEV),), device_id_type=MESH)

    for k in range(1, N_DEV):
        dg_copy(k).start()
    h_copy = pltpu.make_async_copy(hs, h_hbm, h_sem)
    h_copy.start()
    c2, c3 = CHUNKS - 2, CHUNKS - 1
    rs_finish(c2, 0, 1)
    rs_finish(c3, 1, 0)
    rs_finish(c2, 1, 1)
    rs_finish(c3, 0, 1)
    rs_finish(c3, 1, 1)
    for k in range(1, N_DEV):
        dg_copy(k).wait()
    dg_out[...] = functools.reduce(jnp.add, [dgrx[k] for k in range(1, N_DEV)], dgv[...]) / LOGIT_SCALE
    loss_out[...] = jnp.broadcast_to(jnp.sum(lossv[...], axis=1, keepdims=True) / mask_total, loss_out.shape)
    rs_finish(c2, 0, 2)
    rs_finish(c2, 1, 2)
    rs_finish(c3, 0, 2)
    rs_finish(c3, 1, 2)
    for c in range(CHUNKS):
        dh = acc[c, yc, xc, core] / LOGIT_SCALE
        piece = core + 2 * xc + 4 * yc
        inv = rcol[c, piece][:, 0:1]
        xh = xv[c, piece].astype(F32) * inv
        u = dh * g_in[...]
        dx_out[c * PIECE:(c + 1) * PIECE, :] = inv * (u - xh * jnp.mean(u * xh, axis=1, keepdims=True))
    h_copy.wait()
    dz_out(c2).wait()
    dz_out(c3).wait()


def table_grad_kernel(dz, h, dx_in, dg_in, loss_in, de_out, dx_out, dg_out, loss_out):
    de_out[...] = jnp.dot(dz[...], h[...], preferred_element_type=F32) * (1.0 / LOGIT_SCALE)

    @pl.when(pl.program_id(0) == 0)
    def _():
        dx_out[...] = dx_in[...]
        dg_out[...] = dg_in[...]
        loss_out[...] = loss_in[...]


def solution(mesh):
    vp_axis = mesh.axis_names[0]
    vmem = pl.BlockSpec(memory_space=pltpu.VMEM)
    anywhere = pl.BlockSpec(memory_space=pl.ANY)
    dma = pltpu.SemaphoreType.DMA

    def local_step(residual, labels, loss_mask, norm_gain, table_shard):
        max_tile = max(n for _, n in TILES)
        dz, h, dx, dg, loss = pl.pallas_call(
            main_kernel,
            out_shape=(
                jax.ShapeDtypeStruct((ROWS, TOKENS), BF16),
                jax.ShapeDtypeStruct((CHUNKS, CTOK, DIM), BF16),
                jax.ShapeDtypeStruct((TOKENS // N_DEV, DIM), F32),
                jax.ShapeDtypeStruct((1, DIM), F32),
                jax.ShapeDtypeStruct((1, 128), F32),
            ),
            in_specs=[anywhere, vmem, vmem, vmem, anywhere],
            out_specs=(anywhere, anywhere, vmem, vmem, vmem),
            scratch_shapes=[
                pltpu.VMEM((ROWS, DIM), BF16),
                pltpu.VMEM((CHUNKS, N_DEV, PIECE, DIM), BF16),
                pltpu.VMEM((CHUNKS, CTOK, DIM), BF16),
                pltpu.VMEM((CHUNKS, DIM, CTOK), BF16),
                pltpu.VMEM((CHUNKS, N_DEV, PIECE, 128), F32),
                pltpu.VMEM((2, ROWS, CTOK), F32),
                pltpu.VMEM((2, ROWS, CTOK), BF16),
                pltpu.VMEM((CHUNKS, 2, 2, 2, PIECE, DIM), F32),
                pltpu.VMEM((max_tile, CTOK), F32),
                pltpu.VMEM((max_tile, CTOK), F32),
                pltpu.VMEM((CHUNKS, 1, CTOK), jnp.int32),
                pltpu.VMEM((CHUNKS, 1, CTOK), F32),
                pltpu.VMEM((2, N_TILES, CTOK), F32),
                pltpu.VMEM((2, N_TILES, CTOK), F32),
                pltpu.VMEM((N_TILES, CTOK), F32),
                pltpu.VMEM((8, CTOK), F32),
                pltpu.VMEM((CHUNKS, 8, CTOK), F32),
                pltpu.VMEM((CHUNKS, N_DEV, 8, CTOK), F32),
                pltpu.VMEM((1, CTOK), F32),
                pltpu.VMEM((1, DIM), F32),
                pltpu.VMEM((N_DEV, 1, DIM), F32),
                pltpu.VMEM((CHUNKS, 2, 2, 2, PIECE, HALF), F32),
                pltpu.VMEM((CHUNKS, 2, 2, PIECE, HALF), F32),
                pltpu.VMEM((CHUNKS, 2, PIECE, HALF), F32),
                dma((6,)),
                dma,
                dma((2,)),
                dma((CHUNKS, N_DEV)),
                dma((CHUNKS, N_DEV)),
                dma((CHUNKS, 2, 3)),
                dma((CHUNKS, 2, 3)),
                dma((N_DEV,)),
                dma((N_DEV,)),
            ],
            compiler_params=pltpu.CompilerParams(collective_id=0, has_side_effects=True, vmem_limit_bytes=60 << 20),
            cost_estimate=pl.CostEstimate(flops=4 * ROWS * TOKENS * DIM, bytes_accessed=30 << 20, transcendentals=ROWS * TOKENS),
        )(
            residual.reshape(N_DEV, CHUNKS, PIECE, DIM),
            labels.reshape(N_DEV, 128),
            loss_mask.reshape(N_DEV, 128),
            norm_gain.reshape(1, DIM),
            table_shard,
        )
        block = 784
        whole = lambda shape: pl.BlockSpec(shape, lambda i: (0, 0))
        d_embed, dx, dg, loss = pl.pallas_call(
            table_grad_kernel,
            grid=(pl.cdiv(ROWS, block),),
            out_shape=(
                jax.ShapeDtypeStruct((ROWS, DIM), F32),
                jax.ShapeDtypeStruct(dx.shape, F32),
                jax.ShapeDtypeStruct(dg.shape, F32),
                jax.ShapeDtypeStruct(loss.shape, F32),
            ),
            in_specs=[pl.BlockSpec((block, TOKENS), lambda i: (i, 0)), whole((TOKENS, DIM)), whole(dx.shape), whole(dg.shape), whole(loss.shape)],
            out_specs=(pl.BlockSpec((block, DIM), lambda i: (i, 0)), whole(dx.shape), whole(dg.shape), whole(loss.shape)),
            compiler_params=pltpu.CompilerParams(vmem_limit_bytes=60 << 20),
            cost_estimate=pl.CostEstimate(flops=2 * ROWS * TOKENS * DIM, bytes_accessed=40 << 20, transcendentals=0),
        )(dz, h.reshape(TOKENS, DIM), dx, dg, loss)
        return loss[0, 0], dx, d_embed, dg[0]

    return jax.shard_map(local_step, mesh=mesh, in_specs=(P(), P(), P(), P(), P(vp_axis, None)), out_specs=(P(), P(vp_axis, None), P(vp_axis, None), P()), check_vma=False)
```

time: 207 us -> 80.3 us (0.39)
  Pallas kernels: 0 us -> 79.3 us
  blocking collectives: 70.6 us -> 0 us
  matrix products: 62.5 us -> 0 us
  other arithmetic: 33.1 us -> 0 us
  waiting for transfers between devices: 19.3 us -> 0 us
  between operations: 16.6 us -> 0.64 us
  local copies, waits for them, and re-layouts: 4.66 us -> 0 us
    pallas_call x0 -> x2, Pallas kernels: none -> 79.3 us  [the longest x1 58.1 us: local_step(): pl.pallas_call(main_kernel, out_shape=(jax.ShapeDtypeStruct((ROWS, TOKENS...]
    dot_general x3 -> x0, matrix products: 62.5 us -> none  [the longest x1 23.3 us: local_step(): jnp.einsum('td,vd->tv', hidden, table_shard, preferred_element_type=jnp.f...]
    psum x2 -> x0, blocking collectives: 45.6 us -> none  [the longest x1 23.3 us: local_step(): row_stats = lax.psum(part_stats, vp_axis)]
    pmax x1 -> x0, blocking collectives: 25.1 us -> none  [local_step(): row_max = lax.pmax(jnp.max(logits, axis=-1), vp_axis)]
    reduce_scatter x1 -> x0, waiting for transfers between devices: 19.3 us -> none  [local_step(): lax.psum_scatter(d_part, vp_axis, scatter_dimension=0, tiled=True)]
    reduce_sum x4 -> x0, other arithmetic: 15.7 us -> none  [the longest x1 11.6 us: local_step(): jnp.sum(shifted, axis=-1)]
    convert_element_type x1 -> x0, other arithmetic: 12.3 us -> none  [local_step(): (jnp.where(is_label, row_prob - 1.0, row_prob) * tok_weight[:, None]).ast...]
    unnamed x10 -> x0, local copies, waits for them, and re-layouts: 4.58 us -> none
  transfers between devices with their start and end apart: 1 -> 0, of which waited for: 1 -> 0; matrix products, arithmetic and copies ran while one was open for 11% -> 0% of each run, Pallas kernels for 0% -> 0%
where the time goes in v1:
time: 80.3 us; the launch traced here: 79.9 us
  Pallas kernels  79.3 us (99%)
    pallas_call x1, Pallas kernels, local_step(): pl.pallas_call(main_kernel, out_shape=(jax.ShapeDtypeStruct((ROWS, TOKENS...  58.1 us
    pallas_call x1, Pallas kernels, local_step(): pl.pallas_call(table_grad_kernel, grid=(pl.cdiv(ROWS, block),), out_shape...  21.2 us

profile of v1, /device:TPU:0, one launch (start us, length us, event | category | flops | bytes accessed | tf_op | source)
XLA Modules:
  0.0 79.9 jit_solution(13866587382673277090)
XLA Ops:
  0.6 58.1 %shard_map.84 = (bf16[6176,1024]{1,0:T(8,128)(2,1)}, bf16[4,256,1024]{2,1,0:T(8,128)(2,1)}, f32[128,1024]{1,0:T(8,128)}, f32[1,1024]{1,0:T(1,128)}, f32[1,128]{1,0:T(1,128)}) custom-call(bf16[8,4,32,1024]{3,2,1,0:T(8,128)(2,1)} %bitcast.8, s32[8,128]{1,0:T(8,128)} %bitcast.9, f32[8,128]{1,0:T(8,128)} %bitcast.10, f32[1,1024]{1,0:T(1,128)} %bitcast.11, ...), custom_call_target="tpu_custom_call" | custom-call | flops 25904021504 | bytes 31457280 | tf_op jit(solution)/shard_map/pallas_call | solution.py:387
  58.7 21.2 %shard_map.85 = (f32[6176,1024]{1,0:T(8,128)}, f32[128,1024]{1,0:T(8,128)}, f32[1,1024]{1,0:T(1,128)}, f32[1,128]{1,0:T(1,128)}) custom-call(bf16[6176,1024]{1,0:T(8,128)(2,1)} %get-tuple-element.13.dz, bf16[1024,1024]{1,0:T(8,128)(2,1)} %bitcast.12, f32[128,1024]{1,0:T(8,128)} %get-tuple-element.15.dx_in, f32[1,1024]{1,0:T(1,128)} %get-tuple-element.16.dg_in, ...), custom_call_target="tpu_custom_call" | custom-call | flops 12952010752 | bytes 41943040 | tf_op jit(solution)/shard_map/pallas_call | solution.py:444

commit v2 on v1

--- a/solution.py
+++ b/solution.py
@@ -25,7 +25,8 @@
 HALF = DIM // 2
 L_TILE = 256
 K_TILE = 1024
-DZ_BLOCK = 16
+DZ_BLOCK = 32
+L_BLOCK = 16
 MASK_FROM = VOCAB_REAL - (N_DEV - 1) * ROWS
 EXP_SCALE = LOG2E / LOGIT_SCALE
 
@@ -39,6 +40,9 @@
 TILES = split_rows(L_TILE)
 KTILES = split_rows(K_TILE)
 N_TILES = len(TILES)
+E_SPLIT = (0, 3, 8, 16)
+EARLY = 2
+LATE_ROWS = (CHUNKS - EARLY) * PIECE
 
 
 def fold8(v):
@@ -56,9 +60,9 @@
 
 
 def main_kernel(x_hbm, y_in, m_in, g_in, e_hbm,
-                dz_hbm, h_hbm, dx_out, dg_out, loss_out,
+                dz_hbm, h_hbm, own_out, sx_out, sy_out, sd_out, dg_out, loss_out,
                 emb, xv, hs, ht, rcol, ebuf, dzb, acc, ub0, ub1, yrow, mrow,
-                tmax, tsum, crow, tgt, stx, srx, lossv, dgv, dgrx, ra, rb, rc,
+                tmax, tsum, crow, tgt, stx, srx, lossv, dgv, dgsend, dgrx, ra, rb, rc,
                 in_sem, h_sem, dz_sem, st_send, st_recv, rs_send, rs_recv, dg_send, dg_recv):
     me = lax.axis_index("vp")
     core = lax.rem(me, 2)
@@ -68,15 +72,15 @@
     peer_x = me + 2 - 4 * xc
     peer_y = me + 4 - 8 * yc
 
-    mid_row = TILES[N_TILES // 2][0]
+    e_cuts = [TILES[t][0] for t in E_SPLIT] + [ROWS]
     e_copies = [
-        pltpu.make_async_copy(e_hbm.at[pl.ds(0, mid_row)], emb.at[pl.ds(0, mid_row)], in_sem.at[0]),
-        pltpu.make_async_copy(e_hbm.at[pl.ds(mid_row, ROWS - mid_row)], emb.at[pl.ds(mid_row, ROWS - mid_row)], in_sem.at[1]),
+        pltpu.make_async_copy(e_hbm.at[pl.ds(a, b - a)], emb.at[pl.ds(a, b - a)], in_sem.at[CHUNKS + j])
+        for j, (a, b) in enumerate(zip(e_cuts[:-1], e_cuts[1:]))
     ]
-    x_copies = [pltpu.make_async_copy(x_hbm.at[:, c], xv.at[c], in_sem.at[2 + c]) for c in range(CHUNKS)]
+    x_copies = [pltpu.make_async_copy(x_hbm.at[:, c], xv.at[c], in_sem.at[c]) for c in range(CHUNKS)]
     x_copies[0].start()
-    e_copies[0].start()
-    e_copies[1].start()
+    for copy in e_copies:
+        copy.start()
     for c in range(1, CHUNKS):
         x_copies[c].start()
 
@@ -114,9 +118,9 @@
             hs[c, r * PIECE:(r + 1) * PIECE, :] = (xf * inv * g).astype(BF16)
         ht[c] = hs[c].T
 
-    def logits(c, lo, hi, tg):
+    def logits(c, lo, hi, tg, before=None):
         slot = lax.rem(c, 2)
-        iota = lax.broadcasted_iota(jnp.int32, (8, CTOK), 0)
+        iota = lax.broadcasted_iota(jnp.int32, (L_BLOCK, CTOK), 0)
         y = yrow[c]
         eb = ebuf.at[slot]
         ubs = (ub0, ub1)
@@ -130,22 +134,22 @@
         def post(i):
             s, n = TILES[i]
             u_ref = ubs[i % 2]
-            m8 = jnp.full((8, CTOK), -jnp.inf, F32)
-            for r in range(0, n, 8):
-                u = u_ref[r:r + 8, :]
-                if s + r + 8 > MASK_FROM:
+            top = jnp.full((L_BLOCK, CTOK), -jnp.inf, F32)
+            for r in range(0, n, L_BLOCK):
+                u = u_ref[r:r + L_BLOCK, :]
+                if s + r + L_BLOCK > MASK_FROM:
                     u = jnp.where(iota < limit - (s + r), u, -jnp.inf)
-                    u_ref[r:r + 8, :] = u
-                m8 = jnp.maximum(m8, u)
-            m = jnp.max(m8, axis=0, keepdims=True)
-            s8 = jnp.zeros((8, CTOK), F32)
-            for r in range(0, n, 8):
-                u = u_ref[r:r + 8, :]
+                    u_ref[r:r + L_BLOCK, :] = u
+                top = jnp.maximum(top, u)
+            m = jnp.max(top, axis=0, keepdims=True)
+            s8 = jnp.zeros((L_BLOCK, CTOK), F32)
+            for r in range(0, n, L_BLOCK):
+                u = u_ref[r:r + L_BLOCK, :]
                 e = jnp.exp2((u - m) * EXP_SCALE)
-                eb[s + r:s + r + 8, :] = e
+                eb[s + r:s + r + L_BLOCK, :] = e
                 s8 = s8 + e
                 state[0] = state[0] + jnp.where(iota == (y - (s + r)), u, 0.0)
-                if r % 64 == 56:
+                if r % 64 == 64 - L_BLOCK:
                     yield 1
             tmax[slot, i:i + 1, :] = m
             tsum[slot, i:i + 1, :] = jnp.sum(s8, axis=0, keepdims=True)
@@ -154,6 +158,8 @@
         for _ in mm(lo):
             pass
         for i in range(lo + 1, hi):
+            if before is not None and i in before:
+                before[i]()
             interleave(mm(i), post(i - 1), 6)
         for _ in post(hi - 1):
             pass
@@ -256,20 +262,28 @@
         if stage < 2:
             rs_start(c, half, stage + 1)
 
+    def pair_finish(c, half):
+        rs_copy(c, half, 0).wait()
+        cols = slice(half * HALF, half * HALF + HALF)
+        late = pl.ds(pl.multiple_of((c - EARLY) * PIECE, PIECE), PIECE)
+        mine = pl.ds(pl.multiple_of(c * PIECE, PIECE), PIECE)
+
+        def pair_sum(y, x):
+            return acc[c, y, x, core, :, cols] + ra[c, half, y, x]
+
+        own_out[mine, cols] = pair_sum(yc, xc)
+        sx_out[late, cols] = pair_sum(yc, 1 - xc)
+        sy_out[late, cols] = pair_sum(1 - yc, xc)
+        sd_out[late, cols] = pair_sum(1 - yc, 1 - xc)
+
     def step(s, _):
         lc = jnp.minimum(s, CHUNKS - 1)
-        dc = jnp.maximum(s - 1, 0)
+        dc = s - 1
         pc = jnp.maximum(s - 2, 0)
 
         @pl.when(s < CHUNKS)
         def _():
-            tgt[...] = logits(lc, 0, N_TILES // 2, jnp.zeros((8, CTOK), F32))
-
-        @pl.when(s == 0)
-        def _():
-            e_copies[1].wait()
-            for c in range(1, CHUNKS):
-                x_copies[c].wait()
+            tgt[...] = logits(lc, 0, N_TILES // 2, jnp.zeros((L_BLOCK, CTOK), F32))
 
         @pl.when(jnp.logical_and(s >= 2, s < CHUNKS))
         def _():
@@ -280,100 +294,169 @@
             tg = logits(lc, N_TILES // 2, N_TILES, tgt[...])
             send_stats(lc, tg)
 
-        @pl.when(s < CHUNKS - 1)
-        def _():
-            norm_chunk(s + 1)
+        @pl.when(s == 3)
+        def _():
+            rs_finish(0, 0, 2)
+            rs_finish(0, 1, 2)
+
+        @pl.when(s >= 3)
+        def _():
+            dz_out(dc).wait()
+
+        weight = recv_stats(dc)
+        dz_rows(dc, weight, 0)
+        for k in range(1, len(KTILES)):
+            dz_rows(dc, weight, k)
+            dh_mm(dc, k - 1, 0)
+        dh_mm(dc, len(KTILES) - 1, 0)
+        dz_out(dc).start()
+        rs_start(dc, 0, 0)
+        dg_part(dc, 0)
 
         @pl.when(jnp.logical_and(s >= 2, s < CHUNKS))
         def _():
             rs_finish(pc, 0, 1)
 
-        @pl.when(s >= 1)
-        def _():
-            @pl.when(s >= 3)
-            def _():
-                dz_out(dc).wait()
-            weight = recv_stats(dc)
-            dz_rows(dc, weight, 0)
-            for k in range(1, len(KTILES)):
-                dz_rows(dc, weight, k)
-                dh_mm(dc, k - 1, 0)
-            dh_mm(dc, len(KTILES) - 1, 0)
-            dz_out(dc).start()
-            rs_start(dc, 0, 0)
-            dg_part(dc, 0)
+        @pl.when(s == CHUNKS)
+        def _():
+            pair_finish(CHUNKS - 2, 1)
+            rs_finish(1, 0, 2)
+
+        for k in range(len(KTILES)):
+            dh_mm(dc, k, 1)
+        rs_start(dc, 1, 0)
+        dg_part(dc, 1)
+
+        @pl.when(dc < EARLY)
+        def _():
+            rs_finish(dc, 0, 0)
+
+        @pl.when(dc >= EARLY)
+        def _():
+            pair_finish(dc, 0)
 
         @pl.when(jnp.logical_and(s >= 2, s < CHUNKS))
         def _():
             rs_finish(pc, 1, 1)
-
-        @pl.when(s == CHUNKS)
-        def _():
-            rs_finish(pc, 1, 0)
-
-        @pl.when(s >= 1)
-        def _():
-            for k in range(len(KTILES)):
-                dh_mm(dc, k, 1)
-            rs_start(dc, 1, 0)
-            rs_finish(dc, 0, 0)
-            dg_part(dc, 1)
-
-        @pl.when(jnp.logical_and(s >= 2, s < CHUNKS))
-        def _():
-            rs_finish(pc, 0, 2)
-            rs_finish(pc, 1, 2)
         return 0
 
     x_copies[0].wait()
     norm_chunk(0)
+    e_copies[0].wait()
+
+    def more_rows(j):
+        def run():
+            e_copies[j].wait()
+        return run
+
+    tg0 = logits(0, 0, N_TILES, jnp.zeros((L_BLOCK, CTOK), F32), {E_SPLIT[j]: more_rows(j) for j in range(1, len(E_SPLIT))})
     pl.semaphore_wait(barrier, N_DEV - 1)
-    e_copies[0].wait()
-    lax.fori_loop(0, CHUNKS + 1, step, 0)
-
-    def dg_copy(k):
-        return pltpu.make_async_remote_copy(
-            src_ref=dgv, dst_ref=dgrx.at[k], send_sem=dg_send.at[k], recv_sem=dg_recv.at[k],
-            device_id=(lax.rem(me + k, N_DEV),), device_id_type=MESH)
-
-    for k in range(1, N_DEV):
-        dg_copy(k).start()
+    send_stats(0, tg0)
+    for c in range(1, CHUNKS):
+        x_copies[c].wait()
+        norm_chunk(c)
     h_copy = pltpu.make_async_copy(hs, h_hbm, h_sem)
     h_copy.start()
-    c2, c3 = CHUNKS - 2, CHUNKS - 1
-    rs_finish(c2, 0, 1)
-    rs_finish(c3, 1, 0)
-    rs_finish(c2, 1, 1)
-    rs_finish(c3, 0, 1)
-    rs_finish(c3, 1, 1)
-    for k in range(1, N_DEV):
-        dg_copy(k).wait()
-    dg_out[...] = functools.reduce(jnp.add, [dgrx[k] for k in range(1, N_DEV)], dgv[...]) / LOGIT_SCALE
+    lax.fori_loop(1, CHUNKS + 1, step, 0)
+
+    dgsend[...] = dgv[...]
+    dg_copy = pltpu.make_async_remote_copy(
+        src_ref=dgsend, dst_ref=dgrx, send_sem=dg_send, recv_sem=dg_recv, device_id=(peer_core,), device_id_type=MESH)
+    dg_copy.start()
     loss_out[...] = jnp.broadcast_to(jnp.sum(lossv[...], axis=1, keepdims=True) / mask_total, loss_out.shape)
-    rs_finish(c2, 0, 2)
-    rs_finish(c2, 1, 2)
-    rs_finish(c3, 0, 2)
-    rs_finish(c3, 1, 2)
+    rs_finish(1, 1, 2)
+    for c in range(EARLY):
+        own_out[c * PIECE:(c + 1) * PIECE, :] = acc[c, yc, xc, core]
+    pair_finish(CHUNKS - 1, 1)
+    dg_copy.wait()
+    dg_pair = dgv[...] + dgrx[...]
+    dg_out[...] = dg_pair
+    for out in (sx_out, sy_out, sd_out):
+        out[LATE_ROWS:LATE_ROWS + 8, :] = jnp.broadcast_to(dg_pair, (8, DIM))
+    h_copy.wait()
+    dz_out(CHUNKS - 2).wait()
+    dz_out(CHUNKS - 1).wait()
+
+
+def norm_grad_kernel(own, rx, ry, rd, dg_pair, g_in, x_hbm, dx_out, dg_out, x, sem):
+    copy = pltpu.make_async_copy(x_hbm.at[lax.axis_index("vp")], x, sem)
+    copy.start()
+    dg_out[...] = (dg_pair[...] + rx[LATE_ROWS:LATE_ROWS + 1, :] + ry[LATE_ROWS:LATE_ROWS + 1, :] + rd[LATE_ROWS:LATE_ROWS + 1, :]) / LOGIT_SCALE
+    copy.wait()
     for c in range(CHUNKS):
-        dh = acc[c, yc, xc, core] / LOGIT_SCALE
-        piece = core + 2 * xc + 4 * yc
-        inv = rcol[c, piece][:, 0:1]
-        xh = xv[c, piece].astype(F32) * inv
-        u = dh * g_in[...]
-        dx_out[c * PIECE:(c + 1) * PIECE, :] = inv * (u - xh * jnp.mean(u * xh, axis=1, keepdims=True))
+        rows = slice(c * PIECE, (c + 1) * PIECE)
+        dh = own[rows, :]
+        if c >= EARLY:
+            late = slice((c - EARLY) * PIECE, (c - EARLY + 1) * PIECE)
+            dh = dh + rx[late, :] + ry[late, :] + rd[late, :]
+        xf = x[rows, :].astype(F32)
+        inv = lax.rsqrt(jnp.mean(xf * xf, axis=1, keepdims=True) + NORM_EPS)
+        xh = xf * inv
+        u = dh / LOGIT_SCALE * g_in[...]
+        dx_out[rows, :] = inv * (u - xh * jnp.mean(u * xh, axis=1, keepdims=True))
+
+
+D_FIRST, D_STEP, D_RING = 256, 768, 3
+D_LOOPS = (ROWS - D_FIRST) // D_STEP
+D_REST = ROWS - D_FIRST - D_LOOPS * D_STEP
+
+
+def table_grad_kernel(dz_hbm, h_hbm, de_hbm, dz, h, ring, in_sem, h_sem, out_sem):
+    tail = D_LOOPS + 1
+    tail_row = ROWS - D_REST
+
+    def fetch(i, row, rows):
+        return pltpu.make_async_copy(dz_hbm.at[pl.ds(row, rows)], dz.at[pl.ds(row, rows)], in_sem.at[i])
+
+    def store(slot, row, rows):
+        return pltpu.make_async_copy(ring.at[slot, pl.ds(0, rows)], de_hbm.at[pl.ds(row, rows)], out_sem.at[slot])
+
+    def row_of(i):
+        return pl.multiple_of(D_FIRST + (i - 1) * D_STEP, 16)
+
+    def tile(slot, row, rows):
+        ring[slot, 0:rows, :] = jnp.dot(dz[pl.ds(row, rows), :], h[...], preferred_element_type=F32) * (1.0 / LOGIT_SCALE)
+        store(slot, row, rows).start()
+
+    h_copy = pltpu.make_async_copy(h_hbm, h, h_sem)
+    fetch(0, 0, D_FIRST).start()
+    h_copy.start()
+    for i in (1, 2):
+        fetch(i, D_FIRST + (i - 1) * D_STEP, D_STEP).start()
     h_copy.wait()
-    dz_out(c2).wait()
-    dz_out(c3).wait()
-
-
-def table_grad_kernel(dz, h, dx_in, dg_in, loss_in, de_out, dx_out, dg_out, loss_out):
-    de_out[...] = jnp.dot(dz[...], h[...], preferred_element_type=F32) * (1.0 / LOGIT_SCALE)
-
-    @pl.when(pl.program_id(0) == 0)
-    def _():
-        dx_out[...] = dx_in[...]
-        dg_out[...] = dg_in[...]
-        loss_out[...] = loss_in[...]
+    fetch(0, 0, D_FIRST).wait()
+    tile(0, 0, D_FIRST)
+
+    def body(i, _):
+        slot = lax.rem(i, D_RING)
+        fetch(i, row_of(i), D_STEP).wait()
+
+        @pl.when(i + 2 <= D_LOOPS)
+        def _():
+            fetch(i + 2, row_of(i + 2), D_STEP).start()
+
+        @pl.when(i == D_LOOPS - 1)
+        def _():
+            fetch(tail, tail_row, D_REST).start()
+
+        @pl.when(i == D_RING)
+        def _():
+            store(slot, 0, D_FIRST).wait()
+
+        @pl.when(i > D_RING)
+        def _():
+            store(slot, 0, D_STEP).wait()
+
+        tile(slot, row_of(i), D_STEP)
+        return 0
+
+    lax.fori_loop(1, D_LOOPS + 1, body, 0)
+    fetch(tail, tail_row, D_REST).wait()
+    store(tail % D_RING, 0, D_STEP).wait()
+    tile(tail % D_RING, tail_row, D_REST)
+    for i in range(tail - D_RING + 1, tail):
+        store(i % D_RING, 0, D_STEP).wait()
+    store(tail % D_RING, 0, D_REST).wait()
 
 
 def solution(mesh):
@@ -384,17 +467,18 @@
 
     def local_step(residual, labels, loss_mask, norm_gain, table_shard):
         max_tile = max(n for _, n in TILES)
-        dz, h, dx, dg, loss = pl.pallas_call(
+        dz, h, own, sx, sy, sd, dg_pair, loss = pl.pallas_call(
             main_kernel,
             out_shape=(
                 jax.ShapeDtypeStruct((ROWS, TOKENS), BF16),
                 jax.ShapeDtypeStruct((CHUNKS, CTOK, DIM), BF16),
                 jax.ShapeDtypeStruct((TOKENS // N_DEV, DIM), F32),
+                *[jax.ShapeDtypeStruct((LATE_ROWS + 8, DIM), F32)] * 3,
                 jax.ShapeDtypeStruct((1, DIM), F32),
                 jax.ShapeDtypeStruct((1, 128), F32),
             ),
             in_specs=[anywhere, vmem, vmem, vmem, anywhere],
-            out_specs=(anywhere, anywhere, vmem, vmem, vmem),
+            out_specs=(anywhere, anywhere, vmem, vmem, vmem, vmem, vmem, vmem),
             scratch_shapes=[
                 pltpu.VMEM((ROWS, DIM), BF16),
                 pltpu.VMEM((CHUNKS, N_DEV, PIECE, DIM), BF16),
@@ -411,24 +495,25 @@
                 pltpu.VMEM((2, N_TILES, CTOK), F32),
                 pltpu.VMEM((2, N_TILES, CTOK), F32),
                 pltpu.VMEM((N_TILES, CTOK), F32),
-                pltpu.VMEM((8, CTOK), F32),
+                pltpu.VMEM((L_BLOCK, CTOK), F32),
                 pltpu.VMEM((CHUNKS, 8, CTOK), F32),
                 pltpu.VMEM((CHUNKS, N_DEV, 8, CTOK), F32),
                 pltpu.VMEM((1, CTOK), F32),
                 pltpu.VMEM((1, DIM), F32),
-                pltpu.VMEM((N_DEV, 1, DIM), F32),
+                pltpu.VMEM((1, DIM), F32),
+                pltpu.VMEM((1, DIM), F32),
                 pltpu.VMEM((CHUNKS, 2, 2, 2, PIECE, HALF), F32),
-                pltpu.VMEM((CHUNKS, 2, 2, PIECE, HALF), F32),
-                pltpu.VMEM((CHUNKS, 2, PIECE, HALF), F32),
-                dma((6,)),
+                pltpu.VMEM((EARLY, 2, 2, PIECE, HALF), F32),
+                pltpu.VMEM((EARLY, 2, PIECE, HALF), F32),
+                dma((CHUNKS + len(E_SPLIT),)),
                 dma,
                 dma((2,)),
                 dma((CHUNKS, N_DEV)),
                 dma((CHUNKS, N_DEV)),
                 dma((CHUNKS, 2, 3)),
                 dma((CHUNKS, 2, 3)),
-                dma((N_DEV,)),
-                dma((N_DEV,)),
+                dma,
+                dma,
             ],
             compiler_params=pltpu.CompilerParams(collective_id=0, has_side_effects=True, vmem_limit_bytes=60 << 20),
             cost_estimate=pl.CostEstimate(flops=4 * ROWS * TOKENS * DIM, bytes_accessed=30 << 20, transcendentals=ROWS * TOKENS),
@@ -439,22 +524,33 @@
             norm_gain.reshape(1, DIM),
             table_shard,
         )
-        block = 784
-        whole = lambda shape: pl.BlockSpec(shape, lambda i: (0, 0))
-        d_embed, dx, dg, loss = pl.pallas_call(
+        rx, ry, rd = (lax.ppermute(v, vp_axis, [(i, i ^ k) for i in range(N_DEV)]) for v, k in ((sx, 2), (sy, 4), (sd, 6)))
+        d_embed = pl.pallas_call(
             table_grad_kernel,
-            grid=(pl.cdiv(ROWS, block),),
-            out_shape=(
-                jax.ShapeDtypeStruct((ROWS, DIM), F32),
-                jax.ShapeDtypeStruct(dx.shape, F32),
-                jax.ShapeDtypeStruct(dg.shape, F32),
-                jax.ShapeDtypeStruct(loss.shape, F32),
-            ),
-            in_specs=[pl.BlockSpec((block, TOKENS), lambda i: (i, 0)), whole((TOKENS, DIM)), whole(dx.shape), whole(dg.shape), whole(loss.shape)],
-            out_specs=(pl.BlockSpec((block, DIM), lambda i: (i, 0)), whole(dx.shape), whole(dg.shape), whole(loss.shape)),
+            out_shape=jax.ShapeDtypeStruct((ROWS, DIM), F32),
+            in_specs=[anywhere, anywhere],
+            out_specs=anywhere,
+            scratch_shapes=[
+                pltpu.VMEM((ROWS, TOKENS), BF16),
+                pltpu.VMEM((TOKENS, DIM), BF16),
+                pltpu.VMEM((D_RING, D_STEP, DIM), F32),
+                dma((D_LOOPS + 2,)),
+                dma,
+                dma((D_RING,)),
+            ],
             compiler_params=pltpu.CompilerParams(vmem_limit_bytes=60 << 20),
             cost_estimate=pl.CostEstimate(flops=2 * ROWS * TOKENS * DIM, bytes_accessed=40 << 20, transcendentals=0),
-        )(dz, h.reshape(TOKENS, DIM), dx, dg, loss)
+        )(dz, h.reshape(TOKENS, DIM))
+        own_rows = TOKENS // N_DEV
+        dx, dg = pl.pallas_call(
+            norm_grad_kernel,
+            out_shape=(jax.ShapeDtypeStruct((own_rows, DIM), F32), jax.ShapeDtypeStruct((1, DIM), F32)),
+            in_specs=[vmem] * 6 + [anywhere],
+            out_specs=(vmem, vmem),
+            scratch_shapes=[pltpu.VMEM((own_rows, DIM), BF16), dma],
+            compiler_params=pltpu.CompilerParams(vmem_limit_bytes=6 << 20),
+            cost_estimate=pl.CostEstimate(flops=20 * own_rows * DIM, bytes_accessed=2 << 20, transcendentals=own_rows),
+        )(own, rx, ry, rd, dg_pair, norm_gain.reshape(1, DIM), residual.reshape(N_DEV, own_rows, DIM))
         return loss[0, 0], dx, d_embed, dg[0]
 
     return jax.shard_map(local_step, mesh=mesh, in_specs=(P(), P(), P(), P(), P(vp_axis, None)), out_specs=(P(), P(vp_axis, None), P(vp_axis, None), P()), check_vma=False)

time: 80.3 us -> 71.6 us (0.89)
  Pallas kernels: 79.3 us -> 66 us
  starting transfers between devices: 0 us -> 3.5 us
  between operations: 0.64 us -> 1.9 us
    pallas_call x1, Pallas kernels: 58.1 us -> 46.4 us  [local_step(): pl.pallas_call(main_kernel, out_shape=(jax.ShapeDtypeStruct((ROWS, TOKENS...]
    ppermute x0 -> x3, starting transfers between devices: none -> 3.5 us  [local_step(): lax.ppermute(v, vp_axis, [(i, i ^ k) for i in range(N_DEV)])]
    pallas_call x1 -> x2, Pallas kernels: 21.2 us -> 19.6 us  [the longest x1 18.5 us: local_step(): pl.pallas_call(table_grad_kernel, out_shape=jax.ShapeDtypeStruct((ROWS, D...]
  transfers between devices with their start and end apart: 0 -> 3, of which waited for: 0 -> 0; matrix products, arithmetic and copies ran while one was open for 0% -> 0% of each run, Pallas kernels for 0% -> 26%
where the time goes in v2:
time: 71.6 us; the launch traced here: 71.4 us
  Pallas kernels  66 us (92%)
  starting transfers between devices  3.5 us (5%)
  between operations  1.9 us (3%)
    pallas_call x1, Pallas kernels, local_step(): pl.pallas_call(main_kernel, out_shape=(jax.ShapeDtypeStruct((ROWS, TOKENS...  46.4 us
    pallas_call x1, Pallas kernels, local_step(): pl.pallas_call(table_grad_kernel, out_shape=jax.ShapeDtypeStruct((ROWS, D...  18.5 us
    ppermute x3, starting transfers between devices, local_step(): lax.ppermute(v, vp_axis, [(i, i ^ k) for i in range(N_DEV)])  3.5 us
  transfers between devices with their start and end apart: 3, of which 0 were waited for; matrix products, arithmetic and copies ran while one was open for 0% of the time, Pallas kernels for 26%

profile of v2, /device:TPU:0, one launch (start us, length us, event | category | flops | bytes accessed | tf_op | source)
XLA Modules:
  0.0 71.4 jit_solution(4886681877684270213)
XLA Ops:
  0.6 46.4 %shard_map.84 = (bf16[6176,1024]{1,0:T(8,128)(2,1)}, bf16[4,256,1024]{2,1,0:T(8,128)(2,1)}, f32[128,1024]{1,0:T(8,128)}, f32[72,1024]{1,0:T(8,128)}, f32[72,1024...) custom-call(bf16[8,4,32,1024]{3,2,1,0:T(8,128)(2,1)} %bitcast.9, s32[8,128]{1,0:T(8,128)} %bitcast.13, ...), custom_call_target="tpu_custom_call" | custom-call | flops 25904021504 | bytes 31457280 | tf_op jit(solution)/shard_map/pallas_call | solution.py:470
  47.0 0.0 collective-permute-start
  47.1 2.1 %collective-permute-start.1 = (f32[72,1024]{1,0:T(8,128)}, f32[72,1024]{1,0:T(8,128)S(1)}, u32[]{:S(2)}, u32[]{:S(2)}) collective-permute-start(f32[72,1024]{1,0:T(8,128)} %get-tuple-element.17), channel_id=1, source_target_pairs={{0,4},{1,5},{2,6},{3,7},{4,0},{5,1},{6,2},{7,3}} | collective-permute-start | bytes 884744 | tf_op jit(solution)/shard_map/ppermute | solution.py:527
  49.1 1.4 %collective-permute-start.2 = (f32[72,1024]{1,0:T(8,128)}, f32[72,1024]{1,0:T(8,128)S(1)}, u32[]{:S(2)}, u32[]{:S(2)}) collective-permute-start(f32[72,1024]{1,0:T(8,128)} %get-tuple-element.18), channel_id=1, source_target_pairs={{0,6},{1,7},{2,4},{3,5},{4,2},{5,3},{6,0},{7,1}} | collective-permute-start | bytes 884744 | tf_op jit(solution)/shard_map/ppermute | solution.py:527
  50.5 0.0 copy-start
  50.5 0.0 copy-start.1
  50.5 0.0 copy-start.2
  50.5 0.0 copy-start.3
  50.5 0.0 copy-start.4
  50.6 18.5 %shard_map.86 = f32[6176,1024]{1,0:T(8,128)} custom-call(bf16[6176,1024]{1,0:T(8,128)(2,1)} %get-tuple-element.21.dz_hbm, bf16[1024,1024]{1,0:T(8,128)(2,1)} %bitcast.16), custom_call_target="tpu_custom_call" | custom-call | flops 12952010752 | bytes 41943040 | tf_op jit(solution)/shard_map/pallas_call | solution.py:528
  69.1 0.0 collective-permute-done.rx
  69.1 0.0 collective-permute-done.1.ry
  69.1 0.0 collective-permute-done.2.rd
  69.1 0.0 copy-done
  69.1 0.0 copy-done.1
  69.1 0.0 copy-done.2
  69.1 0.0 copy-done.3
  69.1 1.1 %shard_map.85 = (f32[128,1024]{1,0:T(8,128)}, f32[1,1024]{1,0:T(1,128)}) custom-call(f32[128,1024]{1,0:T(8,128)S(1)} %copy-done.1, f32[72,1024]{1,0:T(8,128)S(1)} %collective-permute-done.rx, f32[72,1024]{1,0:T(8,128)S(1)} %collective-permute-done.1.ry, f32[72,1024]{1,0:T(8,128)S(1)} %collective-permute-done.2.rd, f32[1,1024]{1,0:T(1,128)S(1)} %copy-done.3, ...), custom_call_target="tpu_custom_call" | custom-call | flops 2621440 | bytes 2097152 | tf_op jit(solution)/shard_map/pallas_call | solution.py:545
  70.2 0.0 copy-done.4
Async XLA Ops:
  47.0 22.0 %collective-permute-start = (f32[72,1024]{1,0:T(8,128)}, f32[72,1024]{1,0:T(8,128)S(1)}, u32[]{:S(2)}, u32[]{:S(2)}) collective-permute-start(f32[72,1024]{1,0:T(8,128)} %get-tuple-element.16), channel_id=1, source_target_pairs={{0,2},{1,3},{2,0},{3,1},{4,6},{5,7},{6,4},{7,5}} | collective-permute-start | bytes 884744 | tf_op jit(solution)/shard_map/ppermute | solution.py:527
  47.1 22.0 %collective-permute-start.1 = (f32[72,1024]{1,0:T(8,128)}, f32[72,1024]{1,0:T(8,128)S(1)}, u32[]{:S(2)}, u32[]{:S(2)}) collective-permute-start(f32[72,1024]{1,0:T(8,128)} %get-tuple-element.17), channel_id=1, source_target_pairs={{0,4},{1,5},{2,6},{3,7},{4,0},{5,1},{6,2},{7,3}} | collective-permute-start | bytes 884744 | tf_op jit(solution)/shard_map/ppermute | solution.py:527
  49.1 20.0 %collective-permute-start.2 = (f32[72,1024]{1,0:T(8,128)}, f32[72,1024]{1,0:T(8,128)S(1)}, u32[]{:S(2)}, u32[]{:S(2)}) collective-permute-start(f32[72,1024]{1,0:T(8,128)} %get-tuple-element.18), channel_id=1, source_target_pairs={{0,6},{1,7},{2,4},{3,5},{4,2},{5,3},{6,0},{7,1}} | collective-permute-start | bytes 884744 | tf_op jit(solution)/shard_map/ppermute | solution.py:527
  50.5 18.6 %copy-start = (bf16[1024,1024]{1,0:T(8,128)(2,1)S(1)}, bf16[1024,1024]{1,0:T(8,128)(2,1)}, u32[]{:S(2)}) copy-start(bf16[1024,1024]{1,0:T(8,128)(2,1)} %param.5) | copy-start | bytes 6291460
  50.5 18.6 %copy-start.1 = (f32[128,1024]{1,0:T(8,128)S(1)}, f32[128,1024]{1,0:T(8,128)}, u32[]{:S(2)}) copy-start(f32[128,1024]{1,0:T(8,128)} %get-tuple-element.15.own) | copy-start | bytes 1572868
  50.5 18.6 %copy-start.2 = (f32[1024]{0:T(1024)S(1)}, f32[1024]{0:T(1024)}, u32[]{:S(2)}) copy-start(f32[1024]{0:T(1024)} %param.8) | copy-start | bytes 12292
  50.5 18.6 %copy-start.3 = (f32[1,1024]{1,0:T(1,128)S(1)}, f32[1,1024]{1,0:T(1,128)}, u32[]{:S(2)}) copy-start(f32[1,1024]{1,0:T(1,128)} %get-tuple-element.19.dg_pair) | copy-start | bytes 12292
  50.5 19.7 %copy-start.4 = (f32[1,128]{1,0:T(1,128)S(1)}, f32[1,128]{1,0:T(1,128)}, u32[]{:S(2)}) copy-start(f32[1,128]{1,0:T(1,128)} %get-tuple-element.14) | copy-start | bytes 1540

commit v3 on v2

--- a/solution.py
+++ b/solution.py
@@ -23,10 +23,11 @@
 CTOK = 256
 PIECE = 32
 HALF = DIM // 2
-L_TILE = 256
+L_TILE = 128
 K_TILE = 1024
 DZ_BLOCK = 32
 L_BLOCK = 16
+LOWEST = float(jnp.finfo(jnp.float32).min)
 MASK_FROM = VOCAB_REAL - (N_DEV - 1) * ROWS
 EXP_SCALE = LOG2E / LOGIT_SCALE
 
@@ -37,10 +38,10 @@
     return [tuple(c) for c in cuts]
 
 
-TILES = split_rows(L_TILE)
+TILES = [(i * L_TILE, L_TILE) for i in range(ROWS // L_TILE)] + [(ROWS // L_TILE * L_TILE, ROWS % L_TILE)]
 KTILES = split_rows(K_TILE)
 N_TILES = len(TILES)
-E_SPLIT = (0, 3, 8, 16)
+E_SPLIT = (0, 6, 16, 32)
 EARLY = 2
 LATE_ROWS = (CHUNKS - EARLY) * PIECE
 
@@ -62,7 +63,7 @@
 def main_kernel(x_hbm, y_in, m_in, g_in, e_hbm,
                 dz_hbm, h_hbm, own_out, sx_out, sy_out, sd_out, dg_out, loss_out,
                 emb, xv, hs, ht, rcol, ebuf, dzb, acc, ub0, ub1, yrow, mrow,
-                tmax, tsum, crow, tgt, stx, srx, lossv, dgv, dgsend, dgrx, ra, rb, rc,
+                tmax, tsum, crow, stx, srx, lossv, dgv, dgsend, dgrx, ra, rb, rc,
                 in_sem, h_sem, dz_sem, st_send, st_recv, rs_send, rs_recv, dg_send, dg_recv):
     me = lax.axis_index("vp")
     core = lax.rem(me, 2)
@@ -109,13 +110,15 @@
     dgv[...] = jnp.zeros_like(dgv)
     limit = VOCAB_REAL - base
 
+    def norm_rows(c, r):
+        xf = xv[c, r].astype(F32)
+        inv = lax.rsqrt(jnp.mean(xf * xf, axis=1, keepdims=True) + NORM_EPS)
+        rcol[c, r] = jnp.broadcast_to(inv, (PIECE, 128))
+        hs[c, r * PIECE:(r + 1) * PIECE, :] = (xf * inv * g_in[...]).astype(BF16)
+
     def norm_chunk(c):
-        g = g_in[...]
         for r in range(CTOK // PIECE):
-            xf = xv[c, r].astype(F32)
-            inv = lax.rsqrt(jnp.mean(xf * xf, axis=1, keepdims=True) + NORM_EPS)
-            rcol[c, r] = jnp.broadcast_to(inv, (PIECE, 128))
-            hs[c, r * PIECE:(r + 1) * PIECE, :] = (xf * inv * g).astype(BF16)
+            norm_rows(c, r)
         ht[c] = hs[c].T
 
     def logits(c, lo, hi, tg, before=None):
@@ -142,6 +145,8 @@
                     u_ref[r:r + L_BLOCK, :] = u
                 top = jnp.maximum(top, u)
             m = jnp.max(top, axis=0, keepdims=True)
+            if s + L_BLOCK > MASK_FROM:
+                m = jnp.maximum(m, LOWEST)
             s8 = jnp.zeros((L_BLOCK, CTOK), F32)
             for r in range(0, n, L_BLOCK):
                 u = u_ref[r:r + L_BLOCK, :]
@@ -283,21 +288,17 @@
 
         @pl.when(s < CHUNKS)
         def _():
-            tgt[...] = logits(lc, 0, N_TILES // 2, jnp.zeros((L_BLOCK, CTOK), F32))
-
-        @pl.when(jnp.logical_and(s >= 2, s < CHUNKS))
-        def _():
-            rs_finish(pc, 1, 0)
-
-        @pl.when(s < CHUNKS)
-        def _():
-            tg = logits(lc, N_TILES // 2, N_TILES, tgt[...])
-            send_stats(lc, tg)
+            send_stats(lc, logits(lc, 0, N_TILES, jnp.zeros((L_BLOCK, CTOK), F32)))
+
+        @pl.when(s == 2)
+        def _():
+            rs_finish(0, 1, 0)
 
         @pl.when(s == 3)
         def _():
+            rs_finish(0, 1, 1)
+            rs_finish(1, 1, 0)
             rs_finish(0, 0, 2)
-            rs_finish(0, 1, 2)
 
         @pl.when(s >= 3)
         def _():
@@ -311,7 +312,6 @@
         dh_mm(dc, len(KTILES) - 1, 0)
         dz_out(dc).start()
         rs_start(dc, 0, 0)
-        dg_part(dc, 0)
 
         @pl.when(jnp.logical_and(s >= 2, s < CHUNKS))
         def _():
@@ -320,10 +320,17 @@
         @pl.when(s == CHUNKS)
         def _():
             pair_finish(CHUNKS - 2, 1)
-            rs_finish(1, 0, 2)
-
+            rs_finish(1, 1, 1)
+
+        nc = jnp.minimum(s + 1, CHUNKS - 1)
         for k in range(len(KTILES)):
             dh_mm(dc, k, 1)
+            if k == 1:
+                dg_part(dc, 0)
+            if k >= 2:
+                norm_rows(nc, 2 * k - 4)
+                norm_rows(nc, 2 * k - 3)
+        ht[nc] = hs[nc].T
         rs_start(dc, 1, 0)
         dg_part(dc, 1)
 
@@ -335,9 +342,13 @@
         def _():
             pair_finish(dc, 0)
 
-        @pl.when(jnp.logical_and(s >= 2, s < CHUNKS))
-        def _():
-            rs_finish(pc, 1, 1)
+        @pl.when(s == 3)
+        def _():
+            rs_finish(0, 1, 2)
+
+        @pl.when(s == CHUNKS)
+        def _():
+            rs_finish(1, 0, 2)
         return 0
 
     x_copies[0].wait()
@@ -354,10 +365,10 @@
     send_stats(0, tg0)
     for c in range(1, CHUNKS):
         x_copies[c].wait()
-        norm_chunk(c)
+    norm_chunk(1)
+    lax.fori_loop(1, CHUNKS + 1, step, 0)
     h_copy = pltpu.make_async_copy(hs, h_hbm, h_sem)
     h_copy.start()
-    lax.fori_loop(1, CHUNKS + 1, step, 0)
 
     dgsend[...] = dgv[...]
     dg_copy = pltpu.make_async_remote_copy(
@@ -495,7 +506,6 @@
                 pltpu.VMEM((2, N_TILES, CTOK), F32),
                 pltpu.VMEM((2, N_TILES, CTOK), F32),
                 pltpu.VMEM((N_TILES, CTOK), F32),
-                pltpu.VMEM((L_BLOCK, CTOK), F32),
                 pltpu.VMEM((CHUNKS, 8, CTOK), F32),
                 pltpu.VMEM((CHUNKS, N_DEV, 8, CTOK), F32),
                 pltpu.VMEM((1, CTOK), F32),

time: 71.6 us -> 67.2 us (0.939)
  Pallas kernels: 66 us -> 61.6 us
    pallas_call x1, Pallas kernels: 46.4 us -> 42 us  [local_step(): pl.pallas_call(main_kernel, out_shape=(jax.ShapeDtypeStruct((ROWS, TOKENS...]
  transfers between devices with their start and end apart: 3 -> 3, of which waited for: 0 -> 0; matrix products, arithmetic and copies ran while one was open for 0% -> 0% of each run, Pallas kernels for 26% -> 28%
where the time goes in v3:
time: 67.2 us; the launch traced here: 67 us
  Pallas kernels  61.6 us (92%)
  starting transfers between devices  3.51 us (5%)
  between operations  1.89 us (3%)
    pallas_call x1, Pallas kernels, local_step(): pl.pallas_call(main_kernel, out_shape=(jax.ShapeDtypeStruct((ROWS, TOKENS...  42 us
    pallas_call x1, Pallas kernels, local_step(): pl.pallas_call(table_grad_kernel, out_shape=jax.ShapeDtypeStruct((ROWS, D...  18.5 us
    ppermute x3, starting transfers between devices, local_step(): lax.ppermute(v, vp_axis, [(i, i ^ k) for i in range(N_DEV)])  3.51 us
  transfers between devices with their start and end apart: 3, of which 0 were waited for; matrix products, arithmetic and copies ran while one was open for 0% of the time, Pallas kernels for 28%

profile of v3, /device:TPU:0, one launch (start us, length us, event | category | flops | bytes accessed | tf_op | source)
XLA Modules:
  0.0 67.0 jit_solution(11688212372682939671)
XLA Ops:
  0.6 42.0 %shard_map.84 = (bf16[6176,1024]{1,0:T(8,128)(2,1)}, bf16[4,256,1024]{2,1,0:T(8,128)(2,1)}, f32[128,1024]{1,0:T(8,128)}, f32[72,1024]{1,0:T(8,128)}, f32[72,1024...) custom-call(bf16[8,4,32,1024]{3,2,1,0:T(8,128)(2,1)} %bitcast.9, s32[8,128]{1,0:T(8,128)} %bitcast.13, ...), custom_call_target="tpu_custom_call" | custom-call | flops 25904021504 | bytes 31457280 | tf_op jit(solution)/shard_map/pallas_call | solution.py:481
  42.6 1.2 %collective-permute-start = (f32[72,1024]{1,0:T(8,128)}, f32[72,1024]{1,0:T(8,128)S(1)}, u32[]{:S(2)}, u32[]{:S(2)}) collective-permute-start(f32[72,1024]{1,0:T(8,128)} %get-tuple-element.16), channel_id=1, source_target_pairs={{0,2},{1,3},{2,0},{3,1},{4,6},{5,7},{6,4},{7,5}} | collective-permute-start | bytes 884744 | tf_op jit(solution)/shard_map/ppermute | solution.py:537
  43.8 1.6 %collective-permute-start.1 = (f32[72,1024]{1,0:T(8,128)}, f32[72,1024]{1,0:T(8,128)S(1)}, u32[]{:S(2)}, u32[]{:S(2)}) collective-permute-start(f32[72,1024]{1,0:T(8,128)} %get-tuple-element.17), channel_id=1, source_target_pairs={{0,4},{1,5},{2,6},{3,7},{4,0},{5,1},{6,2},{7,3}} | collective-permute-start | bytes 884744 | tf_op jit(solution)/shard_map/ppermute | solution.py:537
  45.4 0.7 %collective-permute-start.2 = (f32[72,1024]{1,0:T(8,128)}, f32[72,1024]{1,0:T(8,128)S(1)}, u32[]{:S(2)}, u32[]{:S(2)}) collective-permute-start(f32[72,1024]{1,0:T(8,128)} %get-tuple-element.18), channel_id=1, source_target_pairs={{0,6},{1,7},{2,4},{3,5},{4,2},{5,3},{6,0},{7,1}} | collective-permute-start | bytes 884744 | tf_op jit(solution)/shard_map/ppermute | solution.py:537
  46.1 0.0 copy-start
  46.1 0.0 copy-start.1
  46.1 0.0 copy-start.2
  46.1 0.0 copy-start.3
  46.1 0.0 copy-start.4
  46.1 18.5 %shard_map.86 = f32[6176,1024]{1,0:T(8,128)} custom-call(bf16[6176,1024]{1,0:T(8,128)(2,1)} %get-tuple-element.21.dz_hbm, bf16[1024,1024]{1,0:T(8,128)(2,1)} %bitcast.16), custom_call_target="tpu_custom_call" | custom-call | flops 12952010752 | bytes 41943040 | tf_op jit(solution)/shard_map/pallas_call | solution.py:538
  64.6 0.0 collective-permute-done.rx
  64.6 0.0 collective-permute-done.1.ry
  64.7 0.0 collective-permute-done.2.rd
  64.7 0.0 copy-done
  64.7 0.0 copy-done.1
  64.7 0.0 copy-done.2
  64.7 0.0 copy-done.3
  64.7 1.1 %shard_map.85 = (f32[128,1024]{1,0:T(8,128)}, f32[1,1024]{1,0:T(1,128)}) custom-call(f32[128,1024]{1,0:T(8,128)S(1)} %copy-done.1, f32[72,1024]{1,0:T(8,128)S(1)} %collective-permute-done.rx, f32[72,1024]{1,0:T(8,128)S(1)} %collective-permute-done.1.ry, f32[72,1024]{1,0:T(8,128)S(1)} %collective-permute-done.2.rd, f32[1,1024]{1,0:T(1,128)S(1)} %copy-done.3, ...), custom_call_target="tpu_custom_call" | custom-call | flops 2621440 | bytes 2097152 | tf_op jit(solution)/shard_map/pallas_call | solution.py:555
  65.8 0.0 copy-done.4
Async XLA Ops:
  42.6 22.0 %collective-permute-start = (f32[72,1024]{1,0:T(8,128)}, f32[72,1024]{1,0:T(8,128)S(1)}, u32[]{:S(2)}, u32[]{:S(2)}) collective-permute-start(f32[72,1024]{1,0:T(8,128)} %get-tuple-element.16), channel_id=1, source_target_pairs={{0,2},{1,3},{2,0},{3,1},{4,6},{5,7},{6,4},{7,5}} | collective-permute-start | bytes 884744 | tf_op jit(solution)/shard_map/ppermute | solution.py:537
  43.8 20.8 %collective-permute-start.1 = (f32[72,1024]{1,0:T(8,128)}, f32[72,1024]{1,0:T(8,128)S(1)}, u32[]{:S(2)}, u32[]{:S(2)}) collective-permute-start(f32[72,1024]{1,0:T(8,128)} %get-tuple-element.17), channel_id=1, source_target_pairs={{0,4},{1,5},{2,6},{3,7},{4,0},{5,1},{6,2},{7,3}} | collective-permute-start | bytes 884744 | tf_op jit(solution)/shard_map/ppermute | solution.py:537
  45.4 19.3 %collective-permute-start.2 = (f32[72,1024]{1,0:T(8,128)}, f32[72,1024]{1,0:T(8,128)S(1)}, u32[]{:S(2)}, u32[]{:S(2)}) collective-permute-start(f32[72,1024]{1,0:T(8,128)} %get-tuple-element.18), channel_id=1, source_target_pairs={{0,6},{1,7},{2,4},{3,5},{4,2},{5,3},{6,0},{7,1}} | collective-permute-start | bytes 884744 | tf_op jit(solution)/shard_map/ppermute | solution.py:537
  46.1 18.6 %copy-start = (bf16[1024,1024]{1,0:T(8,128)(2,1)S(1)}, bf16[1024,1024]{1,0:T(8,128)(2,1)}, u32[]{:S(2)}) copy-start(bf16[1024,1024]{1,0:T(8,128)(2,1)} %param.5) | copy-start | bytes 6291460
  46.1 18.6 %copy-start.1 = (f32[128,1024]{1,0:T(8,128)S(1)}, f32[128,1024]{1,0:T(8,128)}, u32[]{:S(2)}) copy-start(f32[128,1024]{1,0:T(8,128)} %get-tuple-element.15.own) | copy-start | bytes 1572868
  46.1 18.6 %copy-start.2 = (f32[1024]{0:T(1024)S(1)}, f32[1024]{0:T(1024)}, u32[]{:S(2)}) copy-start(f32[1024]{0:T(1024)} %param.8) | copy-start | bytes 12292
  46.1 18.6 %copy-start.3 = (f32[1,1024]{1,0:T(1,128)S(1)}, f32[1,1024]{1,0:T(1,128)}, u32[]{:S(2)}) copy-start(f32[1,1024]{1,0:T(1,128)} %get-tuple-element.19.dg_pair) | copy-start | bytes 12292
  46.1 19.7 %copy-start.4 = (f32[1,128]{1,0:T(1,128)S(1)}, f32[1,128]{1,0:T(1,128)}, u32[]{:S(2)}) copy-start(f32[1,128]{1,0:T(1,128)} %get-tuple-element.14) | copy-start | bytes 1540

commit v4 on v3

--- a/solution.py
+++ b/solution.py
@@ -41,7 +41,7 @@
 TILES = [(i * L_TILE, L_TILE) for i in range(ROWS // L_TILE)] + [(ROWS // L_TILE * L_TILE, ROWS % L_TILE)]
 KTILES = split_rows(K_TILE)
 N_TILES = len(TILES)
-E_SPLIT = (0, 6, 16, 32)
+E_SPLIT = (0, 4, 10, 20, 32)
 EARLY = 2
 LATE_ROWS = (CHUNKS - EARLY) * PIECE
 

time: 67.2 us -> 67 us (level)
  no operation moved by 1% of the time
where the time goes in v4:
time: 67 us; the launch traced here: 66.8 us
  Pallas kernels  61.4 us (92%)
  starting transfers between devices  3.51 us (5%)
  between operations  1.89 us (3%)
    pallas_call x1, Pallas kernels, local_step(): pl.pallas_call(main_kernel, out_shape=(jax.ShapeDtypeStruct((ROWS, TOKENS...  41.8 us
    pallas_call x1, Pallas kernels, local_step(): pl.pallas_call(table_grad_kernel, out_shape=jax.ShapeDtypeStruct((ROWS, D...  18.5 us
    ppermute x3, starting transfers between devices, local_step(): lax.ppermute(v, vp_axis, [(i, i ^ k) for i in range(N_DEV)])  3.51 us
  transfers between devices with their start and end apart: 3, of which 0 were waited for; matrix products, arithmetic and copies ran while one was open for 0% of the time, Pallas kernels for 28%

profile of v4, /device:TPU:0, one launch (start us, length us, event | category | flops | bytes accessed | tf_op | source)
XLA Modules:
  0.0 66.8 jit_solution(17942697936773638666)
XLA Ops:
  0.6 41.8 %shard_map.84 = (bf16[6176,1024]{1,0:T(8,128)(2,1)}, bf16[4,256,1024]{2,1,0:T(8,128)(2,1)}, f32[128,1024]{1,0:T(8,128)}, f32[72,1024]{1,0:T(8,128)}, f32[72,1024...) custom-call(bf16[8,4,32,1024]{3,2,1,0:T(8,128)(2,1)} %bitcast.9, s32[8,128]{1,0:T(8,128)} %bitcast.13, ...), custom_call_target="tpu_custom_call" | custom-call | flops 25904021504 | bytes 31457280 | tf_op jit(solution)/shard_map/pallas_call | solution.py:481
  42.4 1.2 %collective-permute-start = (f32[72,1024]{1,0:T(8,128)}, f32[72,1024]{1,0:T(8,128)S(1)}, u32[]{:S(2)}, u32[]{:S(2)}) collective-permute-start(f32[72,1024]{1,0:T(8,128)} %get-tuple-element.16), channel_id=1, source_target_pairs={{0,2},{1,3},{2,0},{3,1},{4,6},{5,7},{6,4},{7,5}} | collective-permute-start | bytes 884744 | tf_op jit(solution)/shard_map/ppermute | solution.py:537
  43.7 1.5 %collective-permute-start.1 = (f32[72,1024]{1,0:T(8,128)}, f32[72,1024]{1,0:T(8,128)S(1)}, u32[]{:S(2)}, u32[]{:S(2)}) collective-permute-start(f32[72,1024]{1,0:T(8,128)} %get-tuple-element.17), channel_id=1, source_target_pairs={{0,4},{1,5},{2,6},{3,7},{4,0},{5,1},{6,2},{7,3}} | collective-permute-start | bytes 884744 | tf_op jit(solution)/shard_map/ppermute | solution.py:537
  45.2 0.7 %collective-permute-start.2 = (f32[72,1024]{1,0:T(8,128)}, f32[72,1024]{1,0:T(8,128)S(1)}, u32[]{:S(2)}, u32[]{:S(2)}) collective-permute-start(f32[72,1024]{1,0:T(8,128)} %get-tuple-element.18), channel_id=1, source_target_pairs={{0,6},{1,7},{2,4},{3,5},{4,2},{5,3},{6,0},{7,1}} | collective-permute-start | bytes 884744 | tf_op jit(solution)/shard_map/ppermute | solution.py:537
  46.0 0.0 copy-start
  46.0 0.0 copy-start.1
  46.0 0.0 copy-start.2
  46.0 0.0 copy-start.3
  46.0 0.0 copy-start.4
  46.0 18.5 %shard_map.86 = f32[6176,1024]{1,0:T(8,128)} custom-call(bf16[6176,1024]{1,0:T(8,128)(2,1)} %get-tuple-element.21.dz_hbm, bf16[1024,1024]{1,0:T(8,128)(2,1)} %bitcast.16), custom_call_target="tpu_custom_call" | custom-call | flops 12952010752 | bytes 41943040 | tf_op jit(solution)/shard_map/pallas_call | solution.py:538
  64.5 0.0 collective-permute-done.rx
  64.5 0.0 collective-permute-done.1.ry
  64.5 0.0 collective-permute-done.2.rd
  64.5 0.0 copy-done
  64.5 0.0 copy-done.1
  64.5 0.0 copy-done.2
  64.5 0.0 copy-done.3
  64.5 1.1 %shard_map.85 = (f32[128,1024]{1,0:T(8,128)}, f32[1,1024]{1,0:T(1,128)}) custom-call(f32[128,1024]{1,0:T(8,128)S(1)} %copy-done.1, f32[72,1024]{1,0:T(8,128)S(1)} %collective-permute-done.rx, f32[72,1024]{1,0:T(8,128)S(1)} %collective-permute-done.1.ry, f32[72,1024]{1,0:T(8,128)S(1)} %collective-permute-done.2.rd, f32[1,1024]{1,0:T(1,128)S(1)} %copy-done.3, ...), custom_call_target="tpu_custom_call" | custom-call | flops 2621440 | bytes 2097152 | tf_op jit(solution)/shard_map/pallas_call | solution.py:555
  65.7 0.0 copy-done.4
Async XLA Ops:
  42.4 22.0 %collective-permute-start = (f32[72,1024]{1,0:T(8,128)}, f32[72,1024]{1,0:T(8,128)S(1)}, u32[]{:S(2)}, u32[]{:S(2)}) collective-permute-start(f32[72,1024]{1,0:T(8,128)} %get-tuple-element.16), channel_id=1, source_target_pairs={{0,2},{1,3},{2,0},{3,1},{4,6},{5,7},{6,4},{7,5}} | collective-permute-start | bytes 884744 | tf_op jit(solution)/shard_map/ppermute | solution.py:537
  43.7 20.8 %collective-permute-start.1 = (f32[72,1024]{1,0:T(8,128)}, f32[72,1024]{1,0:T(8,128)S(1)}, u32[]{:S(2)}, u32[]{:S(2)}) collective-permute-start(f32[72,1024]{1,0:T(8,128)} %get-tuple-element.17), channel_id=1, source_target_pairs={{0,4},{1,5},{2,6},{3,7},{4,0},{5,1},{6,2},{7,3}} | collective-permute-start | bytes 884744 | tf_op jit(solution)/shard_map/ppermute | solution.py:537
  45.2 19.3 %collective-permute-start.2 = (f32[72,1024]{1,0:T(8,128)}, f32[72,1024]{1,0:T(8,128)S(1)}, u32[]{:S(2)}, u32[]{:S(2)}) collective-permute-start(f32[72,1024]{1,0:T(8,128)} %get-tuple-element.18), channel_id=1, source_target_pairs={{0,6},{1,7},{2,4},{3,5},{4,2},{5,3},{6,0},{7,1}} | collective-permute-start | bytes 884744 | tf_op jit(solution)/shard_map/ppermute | solution.py:537
  46.0 18.6 %copy-start = (bf16[1024,1024]{1,0:T(8,128)(2,1)S(1)}, bf16[1024,1024]{1,0:T(8,128)(2,1)}, u32[]{:S(2)}) copy-start(bf16[1024,1024]{1,0:T(8,128)(2,1)} %param.5) | copy-start | bytes 6291460
  46.0 18.6 %copy-start.1 = (f32[128,1024]{1,0:T(8,128)S(1)}, f32[128,1024]{1,0:T(8,128)}, u32[]{:S(2)}) copy-start(f32[128,1024]{1,0:T(8,128)} %get-tuple-element.15.own) | copy-start | bytes 1572868
  46.0 18.6 %copy-start.2 = (f32[1024]{0:T(1024)S(1)}, f32[1024]{0:T(1024)}, u32[]{:S(2)}) copy-start(f32[1024]{0:T(1024)} %param.8) | copy-start | bytes 12292
  46.0 18.6 %copy-start.3 = (f32[1,1024]{1,0:T(1,128)S(1)}, f32[1,1024]{1,0:T(1,128)}, u32[]{:S(2)}) copy-start(f32[1,1024]{1,0:T(1,128)} %get-tuple-element.19.dg_pair) | copy-start | bytes 12292
  46.0 19.7 %copy-start.4 = (f32[1,128]{1,0:T(1,128)S(1)}, f32[1,128]{1,0:T(1,128)}, u32[]{:S(2)}) copy-start(f32[1,128]{1,0:T(1,128)} %get-tuple-element.14) | copy-start | bytes 1540
